TPU v7x, 32 devices: a whole 2x2x4 slice. The times are simulated.
32 devices in a mesh: batch: 8 (over y, x, core), seq: 4 (over z).
Axes of the slice: x: 2, y: 2, z: 4, core: 2. Of those that a mesh axis runs over, the one named last changes fastest.
Arguments:
- tokens: bfloat16 [8, 1024, 1024], P('batch', 'seq'), may hold values from -6 to 6
- doc_starts: int32 [8, 8], P('batch'), may hold values from 0 to 1023, as said below
- attention_gain: bfloat16 [1024], P(('batch', 'seq')), may hold values from 0.5 to 1.5
- attention_shift: bfloat16 [1024], P(('batch', 'seq')), may hold values from -3 to 3
- joint_weight: bfloat16 [1024, 3072], P(('batch', 'seq')), may hold values from -0.25 to 0.25
- joint_bias: bfloat16 [3072], P(('batch', 'seq')), may hold values from -3 to 3
- output_weight: bfloat16 [1024, 1024], P(('batch', 'seq')), may hold values from -0.5 to 0.5
- output_bias: bfloat16 [1024], P(('batch', 'seq')), may hold values from -3 to 3
- feed_gain: bfloat16 [1024], P(('batch', 'seq')), may hold values from 0.5 to 1.5
- feed_shift: bfloat16 [1024], P(('batch', 'seq')), may hold values from -3 to 3
- up_weight: bfloat16 [1024, 4096], P(('batch', 'seq')), may hold values from -0.1875 to 0.1875
- up_bias: bfloat16 [4096], P(('batch', 'seq')), may hold values from -3 to 3
- down_weight: bfloat16 [4096, 1024], P(('batch', 'seq')), may hold values from -0.125 to 0.125
- down_bias: bfloat16 [1024], P(('batch', 'seq')), may hold values from -3 to 3
- cotangent: bfloat16 [8, 1024, 1024], P('batch', 'seq'), may hold values from -6 to 6
Outputs:
- layer_out: bfloat16 [8, 1024, 1024], P('batch', 'seq')
- input_grad: float32 [8, 1024, 1024], P('batch', 'seq')
- attention_gain_grad: float32 [1024], P(('batch', 'seq'))
- attention_shift_grad: float32 [1024], P(('batch', 'seq'))
- joint_weight_grad: float32 [1024, 3072], P(('batch', 'seq'))
- joint_bias_grad: float32 [3072], P(('batch', 'seq'))
- output_weight_grad: float32 [1024, 1024], P(('batch', 'seq'))
- output_bias_grad: float32 [1024], P(('batch', 'seq'))
- feed_gain_grad: float32 [1024], P(('batch', 'seq'))
- feed_shift_grad: float32 [1024], P(('batch', 'seq'))
- up_weight_grad: float32 [1024, 4096], P(('batch', 'seq'))
- up_bias_grad: float32 [4096], P(('batch', 'seq'))
- down_weight_grad: float32 [4096, 1024], P(('batch', 'seq'))
- down_bias_grad: float32 [1024], P(('batch', 'seq'))
Inputs may be any that keep to these rules, and one draw needn't show every extreme that they name: doc_starts[s, 0] is 0, each row does not fall, and its last entry is 1023; a document is the positions from one start to the next.
All inputs are finite; a program needn't handle non-finite values.
Results may differ from a plain program's by a relative error of at most 0.012.
Values may be sent and summed in bfloat16 or wider, within the bound.
A program may use at most 192 MiB of HBM per device.

v0:
```python
import jax
import jax.numpy as jnp
from jax import lax
from jax.sharding import PartitionSpec as P

HEADS = 16
HEAD_DIM = 64
ROT = 16


block_rows = 512


def norm_rows(values, gain, shift):
    centred = values - jnp.mean(values, axis=-1, keepdims=True)
    spread = jnp.mean(centred * centred, axis=-1, keepdims=True)
    return centred * lax.rsqrt(spread + 1e-05) * gain + shift


def both_norms(values, params):
    return (norm_rows(values, params[0], params[1]), norm_rows(values, params[2], params[3]))


def exact_gelu(values):
    return jax.nn.gelu(values, approximate=False)


def angle_tables(places):
    half = ROT // 2
    inverse = 10000.0 ** (-(jnp.arange(half, dtype=jnp.float32) * 2.0) / ROT)
    angles = places.astype(jnp.float32)[:, None] * inverse[None, :]
    return (jnp.cos(angles)[:, None, :], jnp.sin(angles)[:, None, :])


def rotate(vectors, cosine, sine, sign):
    half = ROT // 2
    front = vectors[..., :half]
    behind = vectors[..., half:ROT]
    new_front = front * cosine - sign * behind * sine
    new_behind = behind * cosine + sign * front * sine
    return jnp.concatenate([new_front, new_behind, vectors[..., ROT:]], axis=-1)


def stream_segments(starts, length):
    places = jnp.arange(length, dtype=jnp.int32)
    return jnp.sum((starts[:, None, :] <= places[None, :, None]).astype(jnp.int32), axis=2)


def block_allowed(places, segment, start, rows):
    query_places = lax.dynamic_slice_in_dim(places, start, rows, 0)
    query_segment = lax.dynamic_slice_in_dim(segment, start, rows, 0)
    return (places[None, :] <= query_places[:, None]) & (segment[None, :] == query_segment[:, None])


def forward_stream(parts, segment, scale):
    query = parts[:, 0]
    keys = parts[:, 1]
    values = parts[:, 2]
    full_len = parts.shape[0]
    rows = min(block_rows, full_len)
    places = jnp.arange(full_len, dtype=jnp.int32)

    def forward_one_block(index):
        start = index * rows
        picked = lax.dynamic_slice_in_dim(query, start, rows, 0)
        allowed = block_allowed(places, segment, start, rows)
        scores = (
            jnp.einsum("qhd,khd->hqk", picked, keys, preferred_element_type=jnp.float32) * scale
        )
        masked = jnp.where(allowed[None], scores, -1e30)
        top = jnp.max(masked, axis=-1, keepdims=True)
        weights = jnp.exp(masked - top)
        total = jnp.sum(weights, axis=-1, keepdims=True)
        probs = (weights / total).astype(jnp.bfloat16)
        result = jnp.einsum("hqk,khd->qhd", probs, values, preferred_element_type=jnp.float32)
        return (result, (top + jnp.log(total))[:, :, 0])

    results, sums_log = lax.map(forward_one_block, jnp.arange(full_len // rows, dtype=jnp.int32))
    return (results.reshape(full_len, keys.shape[1], keys.shape[2]), sums_log)


def backward_stream(parts, segment, sums_log, grad_out, scale):
    query = parts[:, 0]
    keys = parts[:, 1]
    values = parts[:, 2]
    full_len = parts.shape[0]
    rows = min(block_rows, full_len)
    places = jnp.arange(full_len, dtype=jnp.int32)

    def backward_one_block(carry, index):
        key_grad, value_grad = carry
        start = index * rows
        picked = lax.dynamic_slice_in_dim(query, start, rows, 0)
        grad_rows = lax.dynamic_slice_in_dim(grad_out, start, rows, 0)
        allowed = block_allowed(places, segment, start, rows)
        scores = (
            jnp.einsum("qhd,khd->hqk", picked, keys, preferred_element_type=jnp.float32) * scale
        )
        masked = jnp.where(allowed[None], scores, -1e30)
        probs = jnp.exp(masked - sums_log[index][:, :, None])
        value_grad = value_grad + jnp.einsum(
            "hqk,qhd->khd",
            probs.astype(jnp.bfloat16),
            grad_rows,
            preferred_element_type=jnp.float32,
        )
        prob_grad = jnp.einsum(
            "qhd,khd->hqk", grad_rows, values, preferred_element_type=jnp.float32
        )
        inner = jnp.sum(probs * prob_grad, axis=-1, keepdims=True)
        score_grad = (probs * (prob_grad - inner)).astype(jnp.bfloat16)
        query_grad = (
            jnp.einsum("hqk,khd->qhd", score_grad, keys, preferred_element_type=jnp.float32) * scale
        )
        key_grad = (
            key_grad
            + jnp.einsum("hqk,qhd->khd", score_grad, picked, preferred_element_type=jnp.float32)
            * scale
        )
        return ((key_grad, value_grad), query_grad.astype(jnp.bfloat16))

    empty = jnp.zeros(keys.shape, jnp.float32)
    (key_grad, value_grad), query_grads = lax.scan(
        backward_one_block, (empty, empty), jnp.arange(full_len // rows, dtype=jnp.int32)
    )
    query_grad = query_grads.reshape(full_len, keys.shape[1], keys.shape[2])
    return jnp.stack(
        [query_grad, key_grad.astype(jnp.bfloat16), value_grad.astype(jnp.bfloat16)], axis=1
    )


def body(
    tokens,
    doc_starts,
    attention_gain,
    attention_shift,
    joint_weight,
    joint_bias,
    output_weight,
    output_bias,
    feed_gain,
    feed_shift,
    up_weight,
    up_bias,
    down_weight,
    down_bias,
    cotangent,
):
    streams, local_len, width = tokens.shape
    count = streams * local_len
    seq_size = lax.axis_size("seq")
    full_len = local_len * seq_size
    local_heads = HEADS // seq_size
    scale = HEAD_DIM ** (-0.5)
    shards = (
        attention_gain,
        attention_shift,
        joint_weight,
        joint_bias,
        output_weight,
        output_bias,
        feed_gain,
        feed_shift,
        up_weight,
        up_bias,
        down_weight,
        down_bias,
    )
    gathered = (
        lax.all_gather(shards[0], ("batch", "seq"), axis=0, tiled=True),
        lax.all_gather(shards[1], ("batch", "seq"), axis=0, tiled=True),
        lax.all_gather(shards[2], ("batch", "seq"), axis=0, tiled=True),
        lax.all_gather(shards[3], ("batch", "seq"), axis=0, tiled=True),
        lax.all_gather(shards[4], ("batch", "seq"), axis=0, tiled=True),
        lax.all_gather(shards[5], ("batch", "seq"), axis=0, tiled=True),
        lax.all_gather(shards[6], ("batch", "seq"), axis=0, tiled=True),
        lax.all_gather(shards[7], ("batch", "seq"), axis=0, tiled=True),
        lax.all_gather(shards[8], ("batch", "seq"), axis=0, tiled=True),
        lax.all_gather(shards[9], ("batch", "seq"), axis=0, tiled=True),
        lax.all_gather(shards[10], ("batch", "seq"), axis=0, tiled=True),
        lax.all_gather(shards[11], ("batch", "seq"), axis=0, tiled=True),
    )
    (
        full_attention_gain,
        full_attention_shift,
        full_joint,
        full_joint_bias,
        full_output,
        full_output_bias,
        full_feed_gain,
        full_feed_shift,
        full_up,
        full_up_bias,
        full_down,
        full_down_bias,
    ) = gathered
    rows_f32 = tokens.reshape(count, width).astype(jnp.float32)
    norm_params = tuple(
        (
            item.astype(jnp.float32)
            for item in (full_attention_gain, full_attention_shift, full_feed_gain, full_feed_shift)
        )
    )
    (first_f32, second_f32), norm_pullback = jax.vjp(both_norms, rows_f32, norm_params)
    first = first_f32.astype(jnp.bfloat16)
    second = second_f32.astype(jnp.bfloat16)
    mixed = jnp.dot(first, full_joint, preferred_element_type=jnp.float32) + full_joint_bias.astype(
        jnp.float32
    )
    mixed = mixed.reshape(streams, local_len, 3, HEADS, HEAD_DIM)
    places = lax.axis_index("seq") * local_len + jnp.arange(local_len, dtype=jnp.int32)
    cosine, sine = angle_tables(places)
    query = rotate(mixed[:, :, 0], cosine, sine, 1.0)
    keys = rotate(mixed[:, :, 1], cosine, sine, 1.0)
    packed = jnp.stack([query, keys, mixed[:, :, 2]], axis=2).astype(jnp.bfloat16)
    packed = packed.reshape(streams, local_len, 3, width)
    head_side = lax.all_to_all(packed, "seq", split_axis=3, concat_axis=1, tiled=True)
    head_side = head_side.reshape(streams, full_len, 3, local_heads, HEAD_DIM)
    segment = stream_segments(doc_starts, full_len)
    results, sums_log = lax.map(
        lambda item: forward_stream(item[0], item[1], scale), (head_side, segment)
    )
    heads_out = results.astype(jnp.bfloat16).reshape(streams, full_len, local_heads * HEAD_DIM)
    merged = lax.all_to_all(heads_out, "seq", split_axis=1, concat_axis=2, tiled=True).reshape(
        count, width
    )
    attention = jnp.dot(
        merged, full_output, preferred_element_type=jnp.float32
    ) + full_output_bias.astype(jnp.float32)
    up = jnp.dot(second, full_up, preferred_element_type=jnp.float32) + full_up_bias.astype(
        jnp.float32
    )
    active_f32, gelu_pullback = jax.vjp(exact_gelu, up)
    active = active_f32.astype(jnp.bfloat16)
    feed = jnp.dot(active, full_down, preferred_element_type=jnp.float32) + full_down_bias.astype(
        jnp.float32
    )
    layer_out = (
        (rows_f32 + attention + feed).astype(jnp.bfloat16).reshape(streams, local_len, width)
    )
    back_joint, back_output, back_up, back_down = (
        lax.all_gather(joint_weight, ("batch", "seq"), axis=0, tiled=True),
        lax.all_gather(output_weight, ("batch", "seq"), axis=0, tiled=True),
        lax.all_gather(up_weight, ("batch", "seq"), axis=0, tiled=True),
        lax.all_gather(down_weight, ("batch", "seq"), axis=0, tiled=True),
    )
    grad = cotangent.reshape(count, width)
    grad_f32 = grad.astype(jnp.float32)
    down_grad = jnp.einsum("tf,td->fd", active, grad, preferred_element_type=jnp.float32)
    bias_sum = jnp.sum(grad_f32, axis=0)
    active_grad = jnp.einsum("td,fd->tf", grad, back_down, preferred_element_type=jnp.float32)
    up_grad = gelu_pullback(active_grad)[0].astype(jnp.bfloat16)
    up_weight_grad = jnp.einsum("td,tf->df", second, up_grad, preferred_element_type=jnp.float32)
    up_bias_grad = jnp.sum(up_grad.astype(jnp.float32), axis=0)
    second_grad = jnp.einsum("tf,df->td", up_grad, back_up, preferred_element_type=jnp.float32)
    output_weight_grad = jnp.einsum("te,td->ed", merged, grad, preferred_element_type=jnp.float32)
    merged_grad = jnp.einsum(
        "td,ed->te", grad, back_output, preferred_element_type=jnp.float32
    ).astype(jnp.bfloat16)
    heads_grad = lax.all_to_all(
        merged_grad.reshape(streams, local_len, width),
        "seq",
        split_axis=2,
        concat_axis=1,
        tiled=True,
    )
    heads_grad = heads_grad.reshape(streams, full_len, local_heads, HEAD_DIM)
    stream_grads = lax.map(
        lambda item: backward_stream(item[0], item[1], item[2], item[3], scale),
        (head_side, segment, sums_log, heads_grad),
    )
    back_packed = stream_grads.reshape(streams, full_len, 3, local_heads * HEAD_DIM)
    token_side = lax.all_to_all(back_packed, "seq", split_axis=1, concat_axis=3, tiled=True)
    token_side = token_side.astype(jnp.float32).reshape(streams, local_len, 3, HEADS, HEAD_DIM)
    query_back = rotate(token_side[:, :, 0], cosine, sine, -1.0)
    keys_back = rotate(token_side[:, :, 1], cosine, sine, -1.0)
    mixed_grad = (
        jnp.stack([query_back, keys_back, token_side[:, :, 2]], axis=2)
        .astype(jnp.bfloat16)
        .reshape(count, 3 * width)
    )
    joint_weight_grad = jnp.einsum(
        "td,te->de", first, mixed_grad, preferred_element_type=jnp.float32
    )
    joint_bias_grad = jnp.sum(mixed_grad.astype(jnp.float32), axis=0)
    first_grad = jnp.einsum("te,de->td", mixed_grad, back_joint, preferred_element_type=jnp.float32)
    rows_grad, norm_grads = norm_pullback((first_grad, second_grad))
    input_grad = (grad_f32 + rows_grad).reshape(streams, local_len, width)
    every = (
        lax.psum_scatter(norm_grads[0], ("batch", "seq"), scatter_dimension=0, tiled=True),
        lax.psum_scatter(norm_grads[1], ("batch", "seq"), scatter_dimension=0, tiled=True),
        lax.psum_scatter(joint_weight_grad, ("batch", "seq"), scatter_dimension=0, tiled=True),
        lax.psum_scatter(joint_bias_grad, ("batch", "seq"), scatter_dimension=0, tiled=True),
        lax.psum_scatter(output_weight_grad, ("batch", "seq"), scatter_dimension=0, tiled=True),
        lax.psum_scatter(bias_sum, ("batch", "seq"), scatter_dimension=0, tiled=True),
        lax.psum_scatter(norm_grads[2], ("batch", "seq"), scatter_dimension=0, tiled=True),
        lax.psum_scatter(norm_grads[3], ("batch", "seq"), scatter_dimension=0, tiled=True),
        lax.psum_scatter(up_weight_grad, ("batch", "seq"), scatter_dimension=0, tiled=True),
        lax.psum_scatter(up_bias_grad, ("batch", "seq"), scatter_dimension=0, tiled=True),
        lax.psum_scatter(down_grad, ("batch", "seq"), scatter_dimension=0, tiled=True),
    )
    summed = (
        every[0],
        every[1],
        every[2],
        every[3],
        every[4],
        every[5],
        every[6],
        every[7],
        every[8],
        every[9],
        every[10],
        every[5],
    )
    return (layer_out, input_grad) + summed


def solution(mesh):
    placed = (
        P("batch", "seq", None),
        P("batch", None),
        P(("batch", "seq")),
        P(("batch", "seq")),
        P(("batch", "seq"), None),
        P(("batch", "seq")),
        P(("batch", "seq"), None),
        P(("batch", "seq")),
        P(("batch", "seq")),
        P(("batch", "seq")),
        P(("batch", "seq"), None),
        P(("batch", "seq")),
        P(("batch", "seq"), None),
        P(("batch", "seq")),
        P("batch", "seq", None),
    )
    return jax.shard_map(
        body,
        mesh=mesh,
        in_specs=placed,
        out_specs=(
            P("batch", "seq", None),
            P("batch", "seq", None),
            P(("batch", "seq")),
            P(("batch", "seq")),
            P(("batch", "seq"), None),
            P(("batch", "seq")),
            P(("batch", "seq"), None),
            P(("batch", "seq")),
            P(("batch", "seq")),
            P(("batch", "seq")),
            P(("batch", "seq"), None),
            P(("batch", "seq")),
            P(("batch", "seq"), None),
            P(("batch", "seq")),
        ),
        check_vma=False,
    )
```

profile of v0, /device:TPU:0, one launch (start us, length us, event | category | flops | bytes accessed | tf_op | source)
XLA Modules:
  0.0 1390.6 jit_solution(17216495872415283659)
XLA Ops:
  15.9 43.0 %all-reduce.15 = (bf16[1024]{0:T(1024)(128)(2,1)}, bf16[1024]{0:T(1024)(128)(2,1)}, bf16[1024]{0:T(1024)(128)(2,1)}, bf16[3072]{0:T(1024)(128)(2,1)S(1)}, bf16[1...) all-reduce(bf16[1024]{0:T(1024)(128)(2,1)S(1)} %dynamic-update-slic, ...), channel_id=1, replica_groups=mesh['batch'=8,'seq'=4] {'batch','seq'}, use_global_device_ids=true, to_apply=%add.5 | all-reduce | flops 9216 | bytes 36864
  62.8 20.4 %all-gather.6.cloned.1.call-done = bf16[1024,3072]{1,0:T(8,128)(2,1)} async-done(((bf16[32,3072]{1,0:T(8,128)(2,1)}), bf16[1024,3072]{1,0:T(8,128)(2,1)}) %all-gather.6.cloned.1.call-update) | async-done | bytes 6291472 | tf_op jit(solution)/shard_map/all_gather | solution.py:172
  83.2 6.5 convolution_add_fusion.1
  99.3 62.7 %all-gather.8.cloned.1.call-done = bf16[1024,1024]{1,0:T(8,128)(2,1)} async-done(((bf16[32,1024]{1,0:T(8,128)(2,1)}), bf16[1024,1024]{1,0:T(8,128)(2,1)}) %all-gather.8.cloned.1.call-update) | async-done | bytes 2097168 | tf_op jit(solution)/shard_map/all_gather | solution.py:174
  168.0 4.6 reduce.4
  174.6 4.4 all-to-all-start.2
  181.7 19.6 %while.47 = (s32[]{:T(128)}, bf16[2,512,4,64]{1,3,2,0:T(8,128)(2,1)}, f32[2,4,512]{2,1,0:T(4,128)S(1)}, s32[1024]{0:T(1024)S(1)}, s32[2]{0:T(128)S(1)}, /*index=...) while((s32[]{:T(128)}, ...), condition=%wide.region_6.7_spmd.clone, body=%wide.region_3.6_spmd.clone.sunk | while | flops 563607552 | bytes 33378564 | solution.py:78
  212.3 5.1 all-to-all-start.1
  226.1 21.0 %all-to-all-done.1 = bf16[4,2,32768]{2,1,0:T(2,128)(2,1)S(1)} async-done(((bf16[4,2,32768]{2,1,0:T(2,128)(2,1)}), bf16[4,2,32768]{2,1,0:T(2,128)(2,1)S(1)}, u32[]{:S(2)}, u32[]{:S(2)}) %all-to-all-start.1) | async-done | bytes 524320 | tf_op jit(solution)/shard_map/all_to_all | solution.py:224
  252.2 4.0 fusion.79
  256.3 60.5 %while.48 = (s32[]{:T(128)}, f32[1024,4,64]{0,2,1:T(8,128)S(1)}, f32[1024,4,64]{0,2,1:T(8,128)}, bf16[2,512,4,64]{1,3,2,0:T(8,128)(2,1)}, s32[2]{0:T(128)S(1)}, ...) while((s32[]{:T(128)}, f32[1024,4,64]{0,2,1:T(8,128)S(1)}, ...), condition=%wide.region_11.12_spmd.clone.clone, body=%wide.region_9.11_spmd.clone.clone.sunk | while | flops 1376778240 | bytes 132985744 | solution.py:123
  258.2 4.5 fusion.159
  264.7 5.7 multiply_reduce_fusion.2
  277.7 4.8 fusion.162
  288.0 4.5 fusion.159
  294.5 5.7 multiply_reduce_fusion.2
  307.4 4.8 fusion.162
  312.2 4.6 fusion.161
  324.5 89.1 %all_to_all.54 = bf16[1,1024,3,256]{3,2,0,1:T(4,128)(2,1)S(1)} all-to-all(bf16[1,1024,3,256]{3,2,0,1:T(4,128)(2,1)S(1)} %copy.90), channel_id=1, replica_groups=mesh['batch'=8,'seq'=4] {'seq'}, dimensions={1} | all-to-all | bytes 3145728 | tf_op jit(solution)/shard_map/all_to_all | solution.py:273
  420.6 6.5 fusion.74
  427.8 63.6 %all-gather = bf16[32,1,128]{2,1,0:T(2,128)(2,1)S(1)} all-gather(bf16[1,1,128]{2,1,0:T(2,128)(2,1)S(1)} %bitcast.246), channel_id=1, replica_groups=mesh['batch'=8,'seq'=4] {'batch','seq'}, dimensions={0}, use_global_device_ids=true | all-gather | bytes 8448 | tf_op jit(solution)/shard_map/all_gather | solution.py:179
  491.5 16.2 %multiply_convert_fusion.1 = (bf16[256,4096]{1,0:T(8,128)(2,1)}, f32[256,4096]{1,0:T(8,128)}, f32[256,4096]{1,0:T(8,128)}) fusion(f32[4096]{0:T(1024)S(1)} %bitcast.244, bf16[1024,4096]{1,0:T(8,128)(2,1)} %all-gather.10.cloned.1.call-done, bf16[1,256,1024]{2,1,0:T(8,128)(2,1)S(1)} %copy-done.1, f32[1024]{0:T(1024)S(1)} %convert_element_type.195, ...), kind=kOutput, calls=%fused_computation.49 | convolution fusion | flops 2218262528 | bytes 19425280 | tf_op jit(solution)/shard_map/dot_general | solution.py:230
  507.7 12.2 convert_reduce_fusion
  521.3 9.1 fusion.95
  530.7 10.7 fusion.77
  542.0 6.9 convolution_add_fusion.3
  550.6 6.7 fusion.103
  557.4 5.3 fusion.101
  565.3 41.9 %all-reduce.14 = (f32[1024]{0:T(1024)S(1)}, f32[1024]{0:T(1024)S(1)}, f32[3072]{0:T(1024)S(1)}, f32[1024]{0:T(1024)S(1)}, f32[1024]{0:T(1024)S(1)}, /*index=5*/f32[1024]{0:T(1024)S(1)}, f32[4096]{0:T(1024)S(1)}) all-reduce(f32[1024]{0:T(1024)S(1)} %get-tuple-element.268, ...), channel_id=2, replica_groups=mesh['batch'=8,'seq'=4] {'batch','seq'}, use_global_device_ids=true, to_apply=%region_15.16.clone | all-reduce | flops 12288 | bytes 98304
  610.8 44.7 %reduce-scatter.5.cloned.1.call-done = f32[32,3072]{1,0:T(8,128)} async-done(((f32[1024,3072]{1,0:T(8,128)}), f32[32,3072]{1,0:T(8,128)}) %reduce-scatter.5.cloned.1.call-update) | async-done | bytes 393232 | tf_op jit(solution)/shard_map/reduce_scatter | solution.py:292
  655.5 362.5 %reduce-scatter.9.cloned.1.call-done = f32[32,4096]{1,0:T(8,128)} async-done(((f32[1024,4096]{1,0:T(8,128)}), f32[32,4096]{1,0:T(8,128)}) %reduce-scatter.9.cloned.1.call-update) | async-done | bytes 524304 | tf_op jit(solution)/shard_map/reduce_scatter | solution.py:298
  1018.0 364.8 %reduce-scatter.11.cloned.1.call-done = f32[128,1024]{1,0:T(8,128)} async-done(((f32[4096,1024]{1,0:T(8,128)}), f32[128,1024]{1,0:T(8,128)}) %reduce-scatter.11.cloned.1.call-update) | async-done | bytes 524304 | tf_op jit(solution)/shard_map/reduce_scatter | solution.py:300
  (237 shorter events, 122.2 us)
Async XLA Ops:
  7.2 76.0 %all-gather.6.cloned.1.call-start = ((), (), s32[]{:S(2)}) async-start(), calls=%async_computation.8 | async-start | bytes 6488064 | tf_op jit(solution)/shard_map/all_gather | solution.py:172
  7.9 154.1 %all-gather.8.cloned.1.call-start = ((), (), s32[]{:S(2)}) async-start(), calls=%async_computation.9 | async-start | bytes 2162688 | tf_op jit(solution)/shard_map/all_gather | solution.py:174
  8.7 482.8 %all-gather.10.cloned.1.call-start = ((), (), s32[]{:S(2)}) async-start(), calls=%async_computation.10 | async-start | bytes 8650752 | tf_op jit(solution)/shard_map/all_gather | solution.py:178
  9.4 498.3 %all-gather.12.cloned.1.call-start = ((), (), s32[]{:S(2)}) async-start(), calls=%async_computation.11 | async-start | bytes 8650752 | tf_op jit(solution)/shard_map/all_gather | solution.py:180
  58.8 24.4 %copy-start.13 = (f32[1024]{0:T(1024)}, f32[1024]{0:T(1024)S(1)}, u32[]{:S(2)}) copy-start(f32[1024]{0:T(1024)S(1)} %convert_element_type.186) | copy-start | bytes 12292
  58.8 24.4 %copy-start.15 = (f32[1024]{0:T(1024)}, f32[1024]{0:T(1024)S(1)}, u32[]{:S(2)}) copy-start(f32[1024]{0:T(1024)S(1)} %convert_element_type.187) | copy-start | bytes 12292
  60.2 23.0 %copy-start.17 = (f32[256]{0:T(256)}, f32[256]{0:T(256)S(1)}, u32[]{:S(2)}) copy-start(f32[256]{0:T(256)S(1)} %broadcast_multiply_fusion.1) | copy-start | bytes 3076
  62.1 21.1 %copy-start.21 = (f32[256]{0:T(256)}, f32[256]{0:T(256)S(1)}, u32[]{:S(2)}) copy-start(f32[256]{0:T(256)S(1)} %fusion.94) | copy-start | bytes 3076
  62.8 29.6 %copy-start.19 = (f32[256,8]{0,1:T(8,128)}, f32[256,8]{0,1:T(8,128)S(1)}, u32[]{:S(2)}) copy-start(f32[256,8]{0,1:T(8,128)S(1)} %get-tuple-element.360) | copy-start | bytes 24580
  92.8 6.4 copy-start.30
  92.9 69.1 %copy-start.5 = (bf16[1,256,1024]{2,1,0:T(8,128)(2,1)S(1)}, bf16[1,256,1024]{2,1,0:T(8,128)(2,1)}, u32[]{:S(2)}) copy-start(bf16[1,256,1024]{2,1,0:T(8,128)(2,1)} %param.33) | copy-start | bytes 1572868
  95.6 79.0 %all-to-all-start = ((bf16[1,256,3,1024]{1,2,0,3:T(4,128)(2,1)}), bf16[1,256,3,1024]{1,2,0,3:T(4,128)(2,1)S(1)}, u32[]{:S(2)}, u32[]{:S(2)}) async-start(bf16[1,256,3,1024]{1,2,0,3:T(4,128)(2,1)} %copy.81), calls=%async_computation | async-start | bytes 4194304 | tf_op jit(solution)/shard_map/all_to_all | solution.py:217
  174.6 37.7 %all-to-all-start.2 = ((bf16[4,2,32768]{2,1,0:T(2,128)(2,1)}), bf16[4,2,32768]{2,1,0:T(2,128)(2,1)}, u32[]{:S(2)}, u32[]{:S(2)}) async-start(bf16[4,2,32768]{2,1,0:T(2,128)(2,1)} %reshape.601), calls=%async_computation.2 | async-start | bytes 1048576 | tf_op jit(solution)/shard_map/all_to_all | solution.py:260
  212.3 34.8 %all-to-all-start.1 = ((bf16[4,2,32768]{2,1,0:T(2,128)(2,1)}), bf16[4,2,32768]{2,1,0:T(2,128)(2,1)S(1)}, u32[]{:S(2)}, u32[]{:S(2)}) async-start(bf16[4,2,32768]{2,1,0:T(2,128)(2,1)} %reshape.599), calls=%async_computation.1 | async-start | bytes 1048576 | tf_op jit(solution)/shard_map/all_to_all | solution.py:224
  217.4 393.5 %reduce-scatter.7.cloned.1.call-start = ((), (), s32[]{:S(2)}) async-start(), calls=%async_computation.13 | async-start | bytes 4325376 | tf_op jit(solution)/shard_map/reduce_scatter | solution.py:294
  256.2 399.3 %reduce-scatter.5.cloned.1.call-start = ((), (), s32[]{:S(2)}) async-start(), calls=%async_computation.12 | async-start | bytes 12976128 | tf_op jit(solution)/shard_map/reduce_scatter | solution.py:292
  264.7 5.8 slice-start
  264.7 6.0 slice-start.1
  274.4 8.1 copy-start
  277.7 4.8 copy-start.4
  294.4 5.8 slice-start
  294.4 6.0 slice-start.1
  304.1 8.1 copy-start
  307.4 4.8 copy-start.4
  427.2 590.8 %reduce-scatter.9.cloned.1.call-start = ((), (), s32[]{:S(2)}) async-start(), calls=%async_computation.14 | async-start | bytes 17301504 | tf_op jit(solution)/shard_map/reduce_scatter | solution.py:298
  491.5 16.2 %copy-start.6 = (bf16[1,256,1024]{2,1,0:T(8,128)(2,1)S(1)}, bf16[1,256,1024]{2,1,0:T(8,128)(2,1)}, u32[]{:S(2)}) copy-start(bf16[1,256,1024]{2,1,0:T(8,128)(2,1)} %param.33) | copy-start | bytes 1572868
  530.4 852.4 %reduce-scatter.11.cloned.1.call-start = ((), (), s32[]{:S(2)}) async-start(), calls=%async_computation.15 | async-start | bytes 17301504 | tf_op jit(solution)/shard_map/reduce_scatter | solution.py:300
  542.0 6.9 copy-start.3
  542.0 6.9 copy-start.8
  557.4 5.3 copy-start.25
  557.4 5.3 copy-start.7
  607.3 776.0 %copy-start.32 = (f32[32]{0:T(128)}, f32[32]{0:T(128)S(1)}, u32[]{:S(2)}) copy-start(f32[32]{0:T(128)S(1)} %dynamic-slice.4) | copy-start | bytes 388
  (20 other events, 28.7 us)
Sparse Core Ops, SparseCore 0:
  10.9 72.3 all-gather.5
  86.1 75.7 all-gather.7
  164.9 86.8 all-gather.9
  254.5 76.1 all-gather.11
  333.4 162.0 reduce-scatter.6
  501.9 153.5 reduce-scatter.4
  658.4 359.5 reduce-scatter.8
  1020.9 361.9 reduce-scatter.10
where the time goes:
time: 1400 us; the launch traced here: 1390 us
  waiting for transfers between devices  879 us (63%)
  blocking collectives  238 us (17%)
  matrix products  143 us (10%)
  local copies, waits for them, and re-layouts  62.5 us (4%)
  other arithmetic  32.8 us (2%)
  between operations  15.2 us (1%)
  starting transfers between devices  14 us (1%)
    reduce_scatter x1, waiting for transfers between devices, body(): lax.psum_scatter(down_grad, ('batch', 'seq'), scatter_dimension=0, tiled=...  365 us
    reduce_scatter x1, waiting for transfers between devices, body(): lax.psum_scatter(up_weight_grad, ('batch', 'seq'), scatter_dimension=0, t...  362 us
    all_to_all x1, blocking collectives, body(): lax.all_to_all(back_packed, 'seq', split_axis=1, concat_axis=3, tiled=True)  89.1 us
    unnamed x2, blocking collectives  84.9 us
    all_gather x1, blocking collectives, body(): lax.all_gather(shards[9], ('batch', 'seq'), axis=0, tiled=True)  63.6 us
    all_gather x1, waiting for transfers between devices, body(): lax.all_gather(shards[4], ('batch', 'seq'), axis=0, tiled=True)  62.7 us
    reduce_scatter x1, waiting for transfers between devices, body(): lax.psum_scatter(joint_weight_grad, ('batch', 'seq'), scatter_dimension=0...  44.7 us
  transfers between devices with their start and end apart: 11, of which 6 were waited for; matrix products, arithmetic and copies ran while one was open for 17% of the time, Pallas kernels for 0%

commit v1 on v0

v1 whole, which is shorter than its diff:
```python
import jax
import jax.numpy as jnp
from jax import lax
from jax.sharding import PartitionSpec as P

HEADS = 16
HEAD_DIM = 64
ROT = 16
BLOCK_ROWS = 512
F32 = jnp.float32
BF16 = jnp.bfloat16


def dot(a, b, dims):
    return lax.dot_general(a, b, (dims, ((), ())), preferred_element_type=F32)


def normalised(values):
    centred = values - jnp.mean(values, axis=-1, keepdims=True)
    spread = jnp.mean(centred * centred, axis=-1, keepdims=True)
    scale = lax.rsqrt(spread + 1e-05)
    return centred * scale, scale


def angle_tables(places):
    half = ROT // 2
    inverse = 10000.0 ** (-(jnp.arange(half, dtype=F32) * 2.0) / ROT)
    angles = places.astype(F32)[:, None] * inverse[None, :]
    return (jnp.cos(angles)[:, None, :], jnp.sin(angles)[:, None, :])


def rotate(vectors, cosine, sine, sign):
    half = ROT // 2
    front = vectors[..., :half]
    behind = vectors[..., half:ROT]
    new_front = front * cosine - sign * behind * sine
    new_behind = behind * cosine + sign * front * sine
    return jnp.concatenate([new_front, new_behind, vectors[..., ROT:]], axis=-1)


def allowed_block(places, segment, start, rows):
    query_places = lax.dynamic_slice_in_dim(places, start, rows, 0)
    query_segment = lax.dynamic_slice_in_dim(segment, start, rows, 0)
    return (places[None, :] <= query_places[:, None]) & (segment[None, :] == query_segment[:, None])


def forward_stream(query, keys, values, segment, scale):
    full_len = query.shape[0]
    rows = min(BLOCK_ROWS, full_len)
    places = jnp.arange(full_len, dtype=jnp.int32)

    def one_block(index):
        start = index * rows
        picked = lax.dynamic_slice_in_dim(query, start, rows, 0)
        allowed = allowed_block(places, segment, start, rows)
        scores = jnp.einsum("qhd,khd->hqk", picked, keys, preferred_element_type=F32) * scale
        masked = jnp.where(allowed[None], scores, -1e30)
        top = jnp.max(masked, axis=-1, keepdims=True)
        weights = jnp.exp(masked - top)
        total = jnp.sum(weights, axis=-1, keepdims=True)
        probs = (weights / total).astype(BF16)
        result = jnp.einsum("hqk,khd->qhd", probs, values, preferred_element_type=F32)
        return (result.astype(BF16), (top + jnp.log(total))[:, :, 0])

    results, sums_log = lax.map(one_block, jnp.arange(full_len // rows, dtype=jnp.int32))
    return (results.reshape(query.shape), sums_log)


def backward_stream(query, keys, values, segment, sums_log, grad_out, scale):
    full_len = query.shape[0]
    rows = min(BLOCK_ROWS, full_len)
    places = jnp.arange(full_len, dtype=jnp.int32)

    def one_block(carry, index):
        key_grad, value_grad = carry
        start = index * rows
        picked = lax.dynamic_slice_in_dim(query, start, rows, 0)
        grad_rows = lax.dynamic_slice_in_dim(grad_out, start, rows, 0)
        allowed = allowed_block(places, segment, start, rows)
        scores = jnp.einsum("qhd,khd->hqk", picked, keys, preferred_element_type=F32) * scale
        masked = jnp.where(allowed[None], scores, -1e30)
        probs = jnp.exp(masked - sums_log[index][:, :, None])
        value_grad = value_grad + jnp.einsum(
            "hqk,qhd->khd", probs.astype(BF16), grad_rows, preferred_element_type=F32
        )
        prob_grad = jnp.einsum("qhd,khd->hqk", grad_rows, values, preferred_element_type=F32)
        inner = jnp.sum(probs * prob_grad, axis=-1, keepdims=True)
        score_grad = (probs * (prob_grad - inner)).astype(BF16)
        query_grad = (
            jnp.einsum("hqk,khd->qhd", score_grad, keys, preferred_element_type=F32) * scale
        )
        key_grad = (
            key_grad
            + jnp.einsum("hqk,qhd->khd", score_grad, picked, preferred_element_type=F32) * scale
        )
        return ((key_grad, value_grad), query_grad.astype(BF16))

    empty = jnp.zeros(keys.shape, F32)
    (key_grad, value_grad), query_grads = lax.scan(
        one_block, (empty, empty), jnp.arange(full_len // rows, dtype=jnp.int32)
    )
    return (query_grads.reshape(query.shape), key_grad.astype(BF16), value_grad.astype(BF16))


def body(
    tokens,
    doc_starts,
    attention_gain,
    attention_shift,
    joint_weight,
    joint_bias,
    output_weight,
    output_bias,
    feed_gain,
    feed_shift,
    up_weight,
    up_bias,
    down_weight,
    down_bias,
    cotangent,
):
    streams, local_len, width = tokens.shape
    batch_size, seq_size = lax.axis_size("batch"), lax.axis_size("seq")
    devices = batch_size * seq_size
    seq_index = lax.axis_index("seq")
    full_len = local_len * seq_size
    count = streams * full_len
    local_heads = HEADS // seq_size
    head_width = local_heads * HEAD_DIM
    rows = joint_weight.shape[0]
    hidden_rows = down_weight.shape[0]
    hidden = hidden_rows * batch_size
    scale = HEAD_DIM ** (-0.5)
    both = ("batch", "seq")

    vectors = (
        attention_gain, attention_shift, output_bias, feed_gain, feed_shift, down_bias, joint_bias, up_bias,
    )
    packed = jnp.concatenate(vectors)
    sizes = [v.shape[0] for v in vectors]
    everyone = lax.all_gather(packed[None], both, axis=0, tiled=True)
    parts, at = [], 0
    for size in sizes:
        parts.append(everyone[:, at : at + size].astype(F32))
        at += size
    gain_a, shift_a, bias_o, gain_f, shift_f, bias_d, bias_j, bias_u = parts
    gain_a, shift_a, bias_o, gain_f, shift_f, bias_d, bias_j = (
        v.reshape(-1) for v in (gain_a, shift_a, bias_o, gain_f, shift_f, bias_d, bias_j)
    )
    bias_j = lax.dynamic_index_in_dim(
        bias_j.reshape(3, seq_size, head_width), seq_index, 1, keepdims=False
    ).reshape(-1)
    bias_u = lax.dynamic_index_in_dim(
        bias_u.reshape(batch_size, seq_size, hidden_rows), seq_index, 1, keepdims=False
    ).reshape(-1)

    def column_gather(weight, split):
        moved = lax.all_to_all(split, "seq", split_axis=0, concat_axis=0, tiled=True)
        return lax.all_gather(moved.reshape(seq_size * rows, -1), "batch", axis=0, tiled=True)

    full_tokens = lax.all_gather(tokens, "seq", axis=1, tiled=True).reshape(count, width)
    joint = column_gather(
        joint_weight,
        joint_weight.reshape(rows, 3, seq_size, head_width).transpose(2, 0, 1, 3).reshape(seq_size, rows, -1),
    )
    up_w = column_gather(
        up_weight,
        up_weight.reshape(rows, batch_size, seq_size, hidden_rows)
        .transpose(2, 0, 1, 3)
        .reshape(seq_size, rows, -1),
    )
    down_w = lax.all_gather(down_weight, "batch", axis=0, tiled=True)
    there = []
    for b in range(batch_size):
        for s in range(seq_size):
            r = b * seq_size + s
            there.append((r, (r % batch_size) * seq_size + r // batch_size))
    back = [(d, r) for r, d in there]
    out_w = lax.all_gather(
        lax.ppermute(output_weight, both, there), "batch", axis=0, tiled=True
    )
    grad = lax.all_gather(cotangent, "seq", axis=1, tiled=True).reshape(count, width)

    rows_f32 = full_tokens.astype(F32)
    unit, _ = normalised(rows_f32)
    first = (unit * gain_a + shift_a).astype(BF16)
    second = (unit * gain_f + shift_f).astype(BF16)
    mixed = dot(first, joint, ((1,), (0,))) + bias_j
    mixed = mixed.reshape(streams, full_len, 3, local_heads, HEAD_DIM)
    cosine, sine = angle_tables(jnp.arange(full_len, dtype=jnp.int32))
    query = rotate(mixed[:, :, 0], cosine, sine, 1.0).astype(BF16)
    keys = rotate(mixed[:, :, 1], cosine, sine, 1.0).astype(BF16)
    values = mixed[:, :, 2].astype(BF16)
    places = jnp.arange(full_len, dtype=jnp.int32)
    segment = jnp.sum((doc_starts[:, None, :] <= places[None, :, None]).astype(jnp.int32), axis=2)
    heads_out, sums_log = lax.map(
        lambda item: forward_stream(*item, scale), (query, keys, values, segment)
    )
    merged = heads_out.reshape(count, head_width)
    up = dot(second, up_w, ((1,), (0,))) + bias_u
    active_f32, gelu_pullback = jax.vjp(lambda v: jax.nn.gelu(v, approximate=False), up)
    active = active_f32.astype(BF16)
    partial_out = dot(merged, out_w, ((1,), (0,))) + dot(active, down_w, ((1,), (0,)))
    summed_out = lax.psum_scatter(
        partial_out.astype(BF16).reshape(streams, full_len, width), "seq", scatter_dimension=1, tiled=True
    )
    layer_out = (tokens.astype(F32) + summed_out.astype(F32) + (bias_o + bias_d)).astype(BF16)

    active_grad = dot(grad, down_w, ((1,), (1,)))
    up_grad = gelu_pullback(active_grad)[0].astype(BF16)
    second_grad = dot(up_grad, up_w, ((1,), (1,)))
    down_grad = dot(active, grad, ((0,), (0,)))
    up_weight_grad = dot(second, up_grad, ((0,), (0,)))
    output_weight_grad = dot(merged, grad, ((0,), (0,)))
    heads_grad = dot(grad, out_w, ((1,), (1,))).astype(BF16)
    heads_grad = heads_grad.reshape(streams, full_len, local_heads, HEAD_DIM)
    query_grad, key_grad, value_grad = lax.map(
        lambda item: backward_stream(*item, scale),
        (query, keys, values, segment, sums_log, heads_grad),
    )
    query_back = rotate(query_grad.astype(F32), cosine, sine, -1.0).astype(BF16)
    keys_back = rotate(key_grad.astype(F32), cosine, sine, -1.0).astype(BF16)
    mixed_grad = jnp.stack([query_back, keys_back, value_grad], axis=2).reshape(count, 3 * head_width)
    joint_weight_grad = dot(first, mixed_grad, ((0,), (0,)))
    first_grad = dot(mixed_grad, joint, ((1,), (1,)))

    incoming = first_grad * gain_a + second_grad * gain_f
    incoming = lax.psum_scatter(
        incoming.astype(BF16).reshape(streams, full_len, width), "seq", scatter_dimension=1, tiled=True
    ).astype(F32)
    own_unit, own_scale = normalised(tokens.astype(F32))
    own_term = own_scale * (
        incoming
        - jnp.mean(incoming, axis=-1, keepdims=True)
        - own_unit * jnp.mean(incoming * own_unit, axis=-1, keepdims=True)
    )
    input_grad = cotangent.astype(F32) + own_term

    def scatter_rows(value):
        return lax.psum_scatter(value.astype(BF16), "batch", scatter_dimension=0, tiled=True)

    def column_scatter(value):
        moved = scatter_rows(value).reshape(seq_size, rows, -1)
        return lax.all_to_all(moved, "seq", split_axis=0, concat_axis=0, tiled=True).astype(F32)

    joint_out = (
        column_scatter(joint_weight_grad)
        .reshape(seq_size, rows, 3, head_width)
        .transpose(1, 2, 0, 3)
        .reshape(rows, -1)
    )
    up_out = (
        column_scatter(up_weight_grad)
        .reshape(seq_size, rows, batch_size, hidden_rows)
        .transpose(1, 2, 0, 3)
        .reshape(rows, -1)
    )
    down_out = scatter_rows(down_grad).astype(F32)
    output_out = lax.ppermute(scatter_rows(output_weight_grad), both, back).astype(F32)

    own = (jnp.arange(seq_size) == seq_index).astype(F32)
    joint_bias_sum = jnp.sum(mixed_grad.astype(F32), axis=0).reshape(3, 1, head_width) * own[None, :, None]
    up_bias_sum = jnp.sum(up_grad.astype(F32), axis=0).reshape(batch_size, 1, hidden_rows) * own[None, :, None]
    sums = (
        jnp.sum(first_grad * unit, axis=0),
        jnp.sum(first_grad, axis=0),
        jnp.sum(cotangent.astype(F32), axis=(0, 1)),
        jnp.sum(second_grad * unit, axis=0),
        jnp.sum(second_grad, axis=0),
        joint_bias_sum.reshape(-1),
        up_bias_sum.reshape(-1),
    )
    grouped = jnp.concatenate([s.reshape(devices, -1) for s in sums], axis=1)
    mine = lax.psum_scatter(grouped, both, scatter_dimension=0, tiled=True)[0]
    small, at = [], 0
    for value in sums:
        size = value.shape[0] // devices
        small.append(mine[at : at + size])
        at += size
    return (
        layer_out,
        input_grad,
        small[0],
        small[1],
        joint_out,
        small[5],
        output_out,
        small[2],
        small[3],
        small[4],
        up_out,
        small[6],
        down_out,
        small[2],
    )


def solution(mesh):
    split = P(("batch", "seq"))
    matrix = P(("batch", "seq"), None)
    rows = P("batch", "seq", None)
    return jax.shard_map(
        body,
        mesh=mesh,
        in_specs=(
            rows, P("batch", None), split, split, matrix, split, matrix, split, split, split, matrix, split,
            matrix, split, rows,
        ),
        out_specs=(
            rows, rows, split, split, matrix, split, matrix, split, split, split, matrix, split, matrix, split,
        ),
        check_vma=False,
    )
```

time: 1400 us -> 526 us (0.38)
  waiting for transfers between devices: 879 us -> 186 us
  blocking collectives: 238 us -> 128 us
  local copies, waits for them, and re-layouts: 62.5 us -> 30.1 us
  matrix products: 143 us -> 113 us
    reduce_scatter x4 -> x6, waiting for transfers between devices: 772 us -> 176 us  [the longest x4 89.5 us: scatter_rows(): lax.psum_scatter(value.astype(BF16), 'batch', scatter_dimension=0, tiled=...]
    all_gather x4 -> x5, waiting for transfers between devices: 83.1 us -> 8.26 us  [the longest x1 8.22 us: body(): lax.all_gather(cotangent, 'seq', axis=1, tiled=True).reshape(count, width)]
    all_to_all x1 -> x2, blocking collectives: 89.1 us -> 33.7 us  [column_gather(): lax.all_to_all(split, 'seq', split_axis=0, concat_axis=0, tiled=True)]
    all_gather x1, blocking collectives: 63.6 us -> 12 us  [body(): lax.all_gather(lax.ppermute(output_weight, both, there), 'batch', axis=0,...]
    dot_general x26, matrix products: 143 us -> 113 us  [the longest x12 63 us: dot(): return lax.dot_general(a, b, (dims, ((), ())), preferred_element_type=F32)]
    unnamed x87 -> x117, local copies, waits for them, and re-layouts: 25.5 us -> 3.65 us
    all_to_all x3 -> x2, waiting for transfers between devices: 21 us -> 0.01 us  [column_scatter(): lax.all_to_all(moved, 'seq', split_axis=0, concat_axis=0, tiled=True)]
  transfers between devices with their start and end apart: 11 -> 15, of which waited for: 6 -> 6; matrix products, arithmetic and copies ran while one was open for 17% -> 31% of each run, Pallas kernels for 0% -> 0%
where the time goes in v1:
time: 526 us; the launch traced here: 522 us
  waiting for transfers between devices  186 us (35%)
  blocking collectives  128 us (24%)
  matrix products  113 us (21%)
  other arithmetic  32.1 us (6%)
  local copies, waits for them, and re-layouts  30.1 us (6%)
  between operations  15.1 us (3%)
  starting transfers between devices  11.4 us (2%)
  loops' own time  7.11 us (1%)
    reduce_scatter x4, waiting for transfers between devices, scatter_rows(): lax.psum_scatter(value.astype(BF16), 'batch', scatter_dimension=0, tiled=...  89.5 us
    unnamed x2, blocking collectives  82.1 us
    dot_general x12, matrix products, dot(): return lax.dot_general(a, b, (dims, ((), ())), preferred_element_type=F32)  63 us
    reduce_scatter x1, waiting for transfers between devices, body(): lax.psum_scatter(partial_out.astype(BF16).reshape(streams, full_len, widt...  43.7 us
    reduce_scatter x1, waiting for transfers between devices, body(): lax.psum_scatter(incoming.astype(BF16).reshape(streams, full_len, width),...  42.6 us
    all_to_all x2, blocking collectives, column_gather(): lax.all_to_all(split, 'seq', split_axis=0, concat_axis=0, tiled=True)  33.7 us
    dot_general x4, matrix products, one_block(): jnp.einsum('qhd,khd->hqk', picked, keys, preferred_element_type=F32) * scale  12.6 us
    all_gather x1, blocking collectives, body(): lax.all_gather(lax.ppermute(output_weight, both, there), 'batch', axis=0,...  12 us
  transfers between devices with their start and end apart: 15, of which 6 were waited for; matrix products, arithmetic and copies ran while one was open for 31% of the time, Pallas kernels for 0%

profile of v1, /device:TPU:0, one launch (start us, length us, event | category | flops | bytes accessed | tf_op | source)
XLA Modules:
  0.0 521.9 jit_solution(6408067850623948157)
XLA Ops:
  9.5 13.8 %all_to_all.20 = bf16[4,32,768]{2,1,0:T(8,128)(2,1)} all-to-all(bf16[4,32,768]{2,1,0:T(8,128)(2,1)S(1)} %reshape.819), channel_id=1, replica_groups=mesh['batch'=8,'seq'=4] {'seq'}, dimensions={0} | all-to-all | bytes 393216 | tf_op jit(solution)/shard_map/all_to_all | solution.py:158
  25.4 19.9 %all_to_all.21 = bf16[4,32,1024]{2,1,0:T(8,128)(2,1)} all-to-all(bf16[4,32,1024]{2,1,0:T(8,128)(2,1)S(1)} %reshape.824), channel_id=1, replica_groups=mesh['batch'=8,'seq'=4] {'seq'}, dimensions={0} | all-to-all | bytes 524288 | tf_op jit(solution)/shard_map/all_to_all | solution.py:158
  46.6 42.3 %all-reduce = bf16[13312]{0:T(1024)(128)(2,1)S(1)} all-reduce(bf16[13312]{0:T(1024)(128)(2,1)S(1)} %dynamic-update-slice), channel_id=2, replica_groups=mesh['batch'=8,'seq'=4] {'batch','seq'}, use_global_device_ids=true, to_apply=%add | all-reduce | flops 13312 | bytes 53248
  90.9 12.0 %all_gather.24 = bf16[256,1024]{1,0:T(8,128)(2,1)} all-gather(bf16[32,1024]{1,0:T(8,128)(2,1)S(1)} %collective-permute-done), channel_id=1, replica_groups=mesh['batch'=8,'seq'=4] {'batch'}, dimensions={0}, use_global_device_ids=true | all-gather | bytes 589824 | tf_op jit(solution)/shard_map/all_gather | solution.py:179
  107.4 3.6 fusion.89
  112.4 19.5 %while.49 = (s32[]{:T(128)}, bf16[2,512,4,64]{1,3,2,0:T(8,128)(2,1)}, f32[2,4,512]{2,1,0:T(4,128)S(1)}, s32[1024]{0:T(1024)S(1)}, s32[2]{0:T(128)S(1)}, /*index=...) while((s32[]{:T(128)}, ...), condition=%wide.region_6.7_spmd.clone, body=%wide.region_3.6_spmd.clone.sunk | while | flops 563738624 | bytes 33116428 | solution.py:65
  131.9 8.2 %all-gather.15.cloned.1.call-done = bf16[1,1024,1024]{2,1,0:T(8,128)(2,1)} async-done(((bf16[1,256,1024]{2,1,0:T(8,128)(2,1)}), bf16[1,1024,1024]{2,1,0:T(8,128)(2,1)}) %all-gather.15.cloned.1.call-update) | async-done | bytes 2097168 | tf_op jit(solution)/shard_map/all_gather | solution.py:182
  144.1 57.9 %while.50 = (s32[]{:T(128)}, f32[1024,4,64]{0,2,1:T(8,128)S(1)}, f32[1024,4,64]{0,2,1:T(8,128)}, bf16[2,512,4,64]{1,3,2,0:T(8,128)(2,1)}, s32[2]{0:T(128)S(1)}, ...) while((s32[]{:T(128)}, f32[1024,4,64]{0,2,1:T(8,128)S(1)}, ...), condition=%wide.region_12.13_spmd.clone.clone, body=%wide.region_10.12_spmd.clone.clone.sunk | while | flops 1376778240 | bytes 128791048 | solution.py:99
  145.6 4.6 fusion.185
  152.8 5.7 %multiply_reduce_fusion.2 = (f32[4,512]{1,0:T(4,128)S(1)}, f32[4,512,1024]{2,1,0:T(8,128)S(1)}) fusion(f32[4,512,1024]{2,1,0:T(8,128)} %fusion.185, f32[4,512]{1,0:T(4,128)S(1)} %dynamic-slice_bitcast_fusion.9, pred[512,1024]{1,0:T(8,128)(4,1)S(1)} %compare_and_fusion.5, bf16[1024,4,64]{0,2,1:T(8,128)(2,1)S(1)} %get-tuple-element.592, ...), kind=kOutput, calls=%fused_computation.17.clone.1 | convolution fusion | flops 278919168 | bytes 18104324 | tf_op jit(solution)/shard_map/while/body/eval_jaxpr/while/body/eval_jaxpr/qhd,khd->hqk/dot_general | solution.py:86
  158.8 3.7 multiply_convert_fusion.3
  165.9 5.1 fusion.187
  174.5 4.6 fusion.185
  181.7 5.7 %multiply_reduce_fusion.2 = (f32[4,512]{1,0:T(4,128)S(1)}, f32[4,512,1024]{2,1,0:T(8,128)S(1)}) fusion(f32[4,512,1024]{2,1,0:T(8,128)} %fusion.185, f32[4,512]{1,0:T(4,128)S(1)} %dynamic-slice_bitcast_fusion.9, pred[512,1024]{1,0:T(8,128)(4,1)S(1)} %compare_and_fusion.5, bf16[1024,4,64]{0,2,1:T(8,128)(2,1)S(1)} %get-tuple-element.592, ...), kind=kOutput, calls=%fused_computation.17.clone.1 | convolution fusion | flops 278919168 | bytes 18104324 | tf_op jit(solution)/shard_map/while/body/eval_jaxpr/while/body/eval_jaxpr/qhd,khd->hqk/dot_general | solution.py:86
  187.7 3.7 multiply_convert_fusion.3
  194.7 5.1 fusion.187
  211.6 3.5 fusion.92
  224.3 15.2 %multiply_convert_fusion.1 = (bf16[1024,1024]{1,0:T(8,128)(2,1)}, f32[1024,1024]{1,0:T(8,128)}, f32[1024,1024]{1,0:T(8,128)}) fusion(f32[1024]{0:T(1024)} %bitcast.269, bf16[1024,1024]{1,0:T(8,128)(2,1)} %all-gather.11.cloned.1.call-done, bf16[1,1024,1024]{2,1,0:T(8,128)(2,1)S(1)} %copy-done.3, f32[1024]{0:T(1024)S(1)} %copy-done.44, ...), kind=kOutput, calls=%fused_computation.72 | convolution fusion | flops 2222981120 | bytes 14700544 | tf_op jit(solution)/shard_map/dot_general | solution.py:15
  239.5 8.4 %convert_reduce_fusion.1 = (f32[1024]{0:T(1024)S(1)}, bf16[1024,1024]{1,0:T(8,128)(2,1)S(1)}) fusion(f32[1024,1024]{1,0:T(8,128)} %get-tuple-element.326, bf16[1024,1024]{1,0:T(8,128)(2,1)} %all-gather.13.cloned.1.call-done, bf16[1,1024,1024]{2,1,0:T(8,128)(2,1)} %all-gather.15.cloned.1.call-done, f32[1024,1024]{1,0:T(8,128)} %get-tuple-element.367, ...), kind=kOutput, calls=%fused_computation.68 | convolution fusion | flops 2165308416 | bytes 14688256 | tf_op jit(solution)/shard_map/dot_general | solution.py:15
  249.3 4.1 convolution_convert_fusion
  253.7 6.0 %fusion.86 = bf16[1024,1024]{1,0:T(8,128)(2,1)} fusion(bf16[1024,1024]{1,0:T(8,128)(2,1)} %get-tuple-element.325, bf16[1,1024,1024]{2,1,0:T(8,128)(2,1)} %all-gather.15.cloned.1.call-done), kind=kOutput, calls=%fused_computation.109 | convolution fusion | flops 2148532224 | bytes 6291456 | tf_op jit(solution)/shard_map/dot_general | solution.py:15
  259.8 3.9 fusion.129
  263.7 5.4 %fusion.125 = (f32[1024]{0:T(1024)S(1)}, f32[1024]{0:T(1024)}, bf16[1,1024,1024]{2,1,0:T(8,128)(2,1)}, f32[1024]{0:T(1024)}, f32[1024]{0:T(1024)}) fusion(f32[1024]{0:T(1024)S(1)} %copy-done.49, f32[1024]{0:T(1024)S(1)} %copy-done.33, bf16[1,1024,1024]{2,1,0:T(8,128)(2,1)S(1)} %copy-done.3, f32[1024]{0:T(1024)S(1)} %copy-done.43, ...), kind=kOutput, calls=%fused_computation.200 | convolution fusion | flops 2161111040 | bytes 12615680 | tf_op jit(solution)/shard_map/dot_general | solution.py:15
  269.2 4.6 fusion.128
  276.8 3.4 all-to-all-start.2
  280.7 9.6 %reduce-scatter.13.cloned.1.call-done = bf16[32,1024]{1,0:T(8,128)(2,1)} async-done(((bf16[256,1024]{1,0:T(8,128)(2,1)}), bf16[32,1024]{1,0:T(8,128)(2,1)}) %reduce-scatter.13.cloned.1.call-update) | async-done | bytes 65552 | tf_op jit(solution)/shard_map/reduce_scatter | solution.py:240
  291.7 42.9 %reduce-scatter.15.cloned.1.call-done = bf16[128,1024]{1,0:T(8,128)(2,1)} async-done(((bf16[1024,1024]{1,0:T(8,128)(2,1)}), bf16[128,1024]{1,0:T(8,128)(2,1)}) %reduce-scatter.15.cloned.1.call-update) | async-done | bytes 262160 | tf_op jit(solution)/shard_map/reduce_scatter | solution.py:240
  334.7 4.8 all-to-all-start.3
  342.2 37.0 %reduce-scatter.17.cloned.1.call-done = bf16[128,1024]{1,0:T(8,128)(2,1)} async-done(((bf16[1024,1024]{1,0:T(8,128)(2,1)}), bf16[128,1024]{1,0:T(8,128)(2,1)}) %reduce-scatter.17.cloned.1.call-update) | async-done | bytes 262160 | tf_op jit(solution)/shard_map/reduce_scatter | solution.py:240
  382.3 42.6 %reduce-scatter.9.cloned.1.call-done = bf16[1,256,1024]{2,1,0:T(8,128)(2,1)} async-done(((bf16[1,1024,1024]{2,1,0:T(8,128)(2,1)}), bf16[1,256,1024]{2,1,0:T(8,128)(2,1)}) %reduce-scatter.9.cloned.1.call-update) | async-done | bytes 524304 | tf_op jit(solution)/shard_map/reduce_scatter | solution.py:228
  426.4 43.7 %reduce-scatter.7.cloned.1.call-done = bf16[1,256,1024]{2,1,0:T(8,128)(2,1)} async-done(((bf16[1,1024,1024]{2,1,0:T(8,128)(2,1)}), bf16[1,256,1024]{2,1,0:T(8,128)(2,1)}) %reduce-scatter.7.cloned.1.call-update) | async-done | bytes 524304 | tf_op jit(solution)/shard_map/reduce_scatter | solution.py:204
  473.1 39.8 %all-reduce.1 = f32[32,384]{1,0:T(8,128)S(1)} all-reduce(f32[32,384]{1,0:T(8,128)S(1)} %concatenate.137), channel_id=5, replica_groups=mesh['batch'=8,'seq'=4] {'batch','seq'}, use_global_device_ids=true, to_apply=%region_23.24.clone | all-reduce | flops 12288 | bytes 98304
  (313 shorter events, 86.9 us)
Async XLA Ops:
  7.2 38.2 %copy-start.61 = (bf16[32,1024]{1,0:T(8,128)(2,1)S(1)}, bf16[32,1024]{1,0:T(8,128)(2,1)}, u32[]{:S(2)}) copy-start(bf16[32,1024]{1,0:T(8,128)(2,1)} %param.25) | copy-start | bytes 196612
  7.2 38.9 %copy-start.50 = (bf16[32]{0:T(256)(128)(2,1)S(1)}, bf16[32]{0:T(256)(128)(2,1)}, u32[]{:S(2)}) copy-start(bf16[32]{0:T(256)(128)(2,1)} %param.21) | copy-start | bytes 196
  7.2 38.9 %copy-start.51 = (bf16[32]{0:T(256)(128)(2,1)S(1)}, bf16[32]{0:T(256)(128)(2,1)}, u32[]{:S(2)}) copy-start(bf16[32]{0:T(256)(128)(2,1)} %param.22) | copy-start | bytes 196
  7.2 38.9 %copy-start.52 = (bf16[32]{0:T(256)(128)(2,1)S(1)}, bf16[32]{0:T(256)(128)(2,1)}, u32[]{:S(2)}) copy-start(bf16[32]{0:T(256)(128)(2,1)} %param.26) | copy-start | bytes 196
  7.2 38.9 %copy-start.53 = (bf16[32]{0:T(256)(128)(2,1)S(1)}, bf16[32]{0:T(256)(128)(2,1)}, u32[]{:S(2)}) copy-start(bf16[32]{0:T(256)(128)(2,1)} %param.27) | copy-start | bytes 196
  7.2 38.9 %copy-start.54 = (bf16[32]{0:T(256)(128)(2,1)S(1)}, bf16[32]{0:T(256)(128)(2,1)}, u32[]{:S(2)}) copy-start(bf16[32]{0:T(256)(128)(2,1)} %param.28) | copy-start | bytes 196
  7.2 38.9 %copy-start.55 = (bf16[32]{0:T(256)(128)(2,1)S(1)}, bf16[32]{0:T(256)(128)(2,1)}, u32[]{:S(2)}) copy-start(bf16[32]{0:T(256)(128)(2,1)} %param.32) | copy-start | bytes 196
  7.3 38.9 %copy-start.56 = (bf16[96]{0:T(256)(128)(2,1)S(1)}, bf16[96]{0:T(256)(128)(2,1)}, u32[]{:S(2)}) copy-start(bf16[96]{0:T(256)(128)(2,1)} %param.24) | copy-start | bytes 580
  7.3 38.9 %copy-start.57 = (bf16[128]{0:T(256)(128)(2,1)S(1)}, bf16[128]{0:T(256)(128)(2,1)}, u32[]{:S(2)}) copy-start(bf16[128]{0:T(256)(128)(2,1)} %param.30) | copy-start | bytes 772
  7.3 83.6 %copy-start.58 = (s32[1,8]{1,0:T(1,128)S(1)}, s32[1,8]{1,0:T(1,128)}, u32[]{:S(2)}) copy-start(s32[1,8]{1,0:T(1,128)} %param.20) | copy-start | bytes 100
  7.3 95.7 %all-gather.7.cloned.1.call-start = ((), (), s32[]{:S(2)}) async-start(), calls=%async_computation.10 | async-start | bytes 2621440 | tf_op jit(solution)/shard_map/all_gather | solution.py:161
  8.0 99.4 %all-gather.9.cloned.1.call-start = ((), (), s32[]{:S(2)}) async-start(), calls=%async_computation.11 | async-start | bytes 1769472 | tf_op jit(solution)/shard_map/all_gather | solution.py:159
  23.3 116.8 %all-gather.15.cloned.1.call-start = ((), (), s32[]{:S(2)}) async-start(), calls=%async_computation.15 | async-start | bytes 2621440 | tf_op jit(solution)/shard_map/all_gather | solution.py:182
  24.1 200.2 %all-gather.11.cloned.1.call-start = ((), (), s32[]{:S(2)}) async-start(), calls=%async_computation.12 | async-start | bytes 2359296 | tf_op jit(solution)/shard_map/all_gather | solution.py:159
  45.3 194.2 %all-gather.13.cloned.1.call-start = ((), (), s32[]{:S(2)}) async-start(), calls=%async_computation.13 | async-start | bytes 2359296 | tf_op jit(solution)/shard_map/all_gather | solution.py:172
  45.4 45.6 %collective-permute-start = (bf16[32,1024]{1,0:T(8,128)(2,1)S(1)}, bf16[32,1024]{1,0:T(8,128)(2,1)S(1)}, u32[]{:S(2)}, u32[]{:S(2)}) collective-permute-start(bf16[32,1024]{1,0:T(8,128)(2,1)S(1)} %copy-done.61), channel_id=1, source_target_pairs={{0,0},{1,4},{2,8},{3,12},{4,16},{5,20},{6,24},{7,28},{8,1},{9,5},{... | collective-permute-start | bytes 196616 | tf_op jit(solution)/shard_map/ppermute | solution.py:180
  46.0 230.7 %reduce-scatter.11.cloned.1.call-start = ((), (), s32[]{:S(2)}) async-start(), calls=%async_computation.17 | async-start | bytes 1769472 | tf_op jit(solution)/shard_map/reduce_scatter | solution.py:240
  89.8 21.2 %copy-start.37 = (f32[1024]{0:T(1024)}, f32[1024]{0:T(1024)S(1)}, u32[]{:S(2)}) copy-start(f32[1024]{0:T(1024)S(1)} %reshape.846) | copy-start | bytes 12292
  89.9 21.1 %copy-start.34 = (f32[1024]{0:T(1024)}, f32[1024]{0:T(1024)S(1)}, u32[]{:S(2)}) copy-start(f32[1024]{0:T(1024)S(1)} %reshape.845) | copy-start | bytes 12292
  112.4 27.8 %copy-start.5 = (bf16[256,1024]{1,0:T(8,128)(2,1)S(1)}, bf16[256,1024]{1,0:T(8,128)(2,1)}, u32[]{:S(2)}) copy-start(bf16[256,1024]{1,0:T(8,128)(2,1)} %all_gather.24) | copy-start | bytes 1572868
  215.1 75.1 %reduce-scatter.13.cloned.1.call-start = ((), (), s32[]{:S(2)}) async-start(), calls=%async_computation.18 | async-start | bytes 589824 | tf_op jit(solution)/shard_map/reduce_scatter | solution.py:240
  224.2 110.5 %reduce-scatter.15.cloned.1.call-start = ((), (), s32[]{:S(2)}) async-start(), calls=%async_computation.19 | async-start | bytes 2359296 | tf_op jit(solution)/shard_map/reduce_scatter | solution.py:240
  253.5 125.6 %reduce-scatter.17.cloned.1.call-start = ((), (), s32[]{:S(2)}) async-start(), calls=%async_computation.20 | async-start | bytes 2359296 | tf_op jit(solution)/shard_map/reduce_scatter | solution.py:240
  259.7 165.2 %reduce-scatter.9.cloned.1.call-start = ((), (), s32[]{:S(2)}) async-start(), calls=%async_computation.16 | async-start | bytes 2621440 | tf_op jit(solution)/shard_map/reduce_scatter | solution.py:228
  269.2 200.9 %reduce-scatter.7.cloned.1.call-start = ((), (), s32[]{:S(2)}) async-start(), calls=%async_computation.14 | async-start | bytes 2621440 | tf_op jit(solution)/shard_map/reduce_scatter | solution.py:204
  276.0 64.4 %copy-start.41 = (f32[1024]{0:T(1024)S(1)}, f32[1024]{0:T(1024)}, u32[]{:S(2)}) copy-start(f32[1024]{0:T(1024)} %get-tuple-element.332) | copy-start | bytes 12292
  276.0 64.4 %copy-start.40 = (f32[1024]{0:T(1024)S(1)}, f32[1024]{0:T(1024)}, u32[]{:S(2)}) copy-start(f32[1024]{0:T(1024)} %get-tuple-element.333) | copy-start | bytes 12292
  276.0 64.5 %copy-start.39 = (f32[1024]{0:T(1024)S(1)}, f32[1024]{0:T(1024)}, u32[]{:S(2)}) copy-start(f32[1024]{0:T(1024)} %get-tuple-element.278) | copy-start | bytes 12292
  276.8 14.9 %all-to-all-start.2 = ((bf16[4,32,768]{2,1,0:T(8,128)(2,1)}), bf16[4,32,768]{2,1,0:T(8,128)(2,1)S(1)}, u32[]{:S(2)}, u32[]{:S(2)}) async-start(bf16[4,32,768]{2,1,0:T(8,128)(2,1)} %bitcast.265), calls=%async_computation.5 | async-start | bytes 393216 | tf_op jit(solution)/shard_map/all_to_all | solution.py:244
  280.6 189.5 %copy-start.12 = (bf16[1,256,1024]{2,1,0:T(8,128)(2,1)S(1)}, bf16[1,256,1024]{2,1,0:T(8,128)(2,1)}, u32[]{:S(2)}) copy-start(bf16[1,256,1024]{2,1,0:T(8,128)(2,1)} %param.33) | copy-start | bytes 1572868
  290.3 49.4 %collective-permute-start.1 = (bf16[32,1024]{1,0:T(8,128)(2,1)}, bf16[32,1024]{1,0:T(8,128)(2,1)S(1)}, u32[]{:S(2)}, u32[]{:S(2)}) collective-permute-start(bf16[32,1024]{1,0:T(8,128)(2,1)} %reduce-scatter.13.cloned.1.call-done), channel_id=1, source_target_pairs={{0,0},{4,1},{8,2},{12,3},{16,4},{20,5},{24,6},{28,7},{1,8},{5,9},{... | collective-permute-start | bytes 196616 | tf_op jit(solution)/shard_map/ppermute | solution.py:259
  334.7 46.2 %all-to-all-start.3 = ((bf16[4,32,1024]{2,1,0:T(8,128)(2,1)}), bf16[4,32,1024]{2,1,0:T(8,128)(2,1)S(1)}, u32[]{:S(2)}, u32[]{:S(2)}) async-start(bf16[4,32,1024]{2,1,0:T(8,128)(2,1)} %bitcast.264), calls=%async_computation.8 | async-start | bytes 524288 | tf_op jit(solution)/shard_map/all_to_all | solution.py:244
  (59 other events, 273.9 us)
Sparse Core Ops, SparseCore 0:
  9.7 56.8 all-gather.6
  68.5 24.5 all-gather.8
  94.6 45.4 all-gather.14
  141.9 26.5 all-gather.10
  170.3 27.7 all-gather.12
  215.2 37.1 reduce-scatter.10
  256.1 34.0 reduce-scatter.12
  293.5 41.1 reduce-scatter.14
  338.0 41.0 reduce-scatter.16
  381.2 43.6 reduce-scatter.8
  427.2 42.8 reduce-scatter.6
